TPU v7x, 32 devices: a whole 2x2x4 slice. The times are simulated.
32 devices in a mesh: group: 2 (over x), dp: 2 (over core), tensor: 8 (over z, y).
Axes of the slice: x: 2, y: 2, z: 4, core: 2. Of those that a mesh axis runs over, the one named last changes fastest.
Arguments:
- teacher_hidden: bfloat16 [1024, 8192], P(('group', 'dp'), 'tensor'), may hold values from -6 to 6
- teacher_gain: float32 [8192], P('tensor'), may hold values from 0.1 to 1.9
- project_weight: bfloat16 [8192, 3584], P('tensor'), may hold values from -0.0625 to 0.0625
- student_hidden: bfloat16 [1024, 3584], P(('group', 'dp', 'tensor')), may hold values from -6 to 6
- student_gain: float32 [3584], replicated, may hold values from 0.1 to 1.9
- gate_weight: bfloat16 [3584, 9472], P(('group', 'dp'), 'tensor'), may hold values from -0.09375 to 0.09375
- up_weight: bfloat16 [3584, 9472], P(('group', 'dp'), 'tensor'), may hold values from -0.09375 to 0.09375
- down_weight: bfloat16 [9472, 3584], P('tensor', ('group', 'dp')), may hold values from -0.0625 to 0.0625
- owner_map: int32 [64, 1], P(('group', 'dp')), may hold values from 0 to 3; in each aligned block of 16 rows (0 to 15, 16 to 31, ...) at most 8 rows name the same one
- token_ids: int32 [1024], P(('group', 'dp', 'tensor')), may hold values from 0 to 511
- token_counts: int32 [64], P(('group', 'dp')), may hold values from 1 to 16
- id_weight: float32 [512], replicated, may hold values from 0.25 to 4
Outputs:
- student_out: bfloat16 [4, 16, 32, 3584], P(('group', 'dp'), 'tensor')
- down_grad: float32 [3584, 9472], P(('group', 'dp'), 'tensor')
Inputs may be any that keep to these rules, and one draw needn't show every extreme that they name: `owner_map`: of the 16 episodes of one index of group and dp (aligned blocks of 16 rows), at most 8 have the same owner; owner o is index o of group and dp in mesh order.
All inputs are finite; a program needn't handle non-finite values.
Results may differ from a plain program's by a relative error of at most 0.02.
Values may be sent and summed in bfloat16 or wider, within the bound.
A program may use at most 128 MiB of HBM per device.

v0:
```python
import math
import jax
import jax.numpy as jnp
from jax import lax
from jax.sharding import PartitionSpec as P

EP_LEN = 16
EXTRA = 128
EPSILON = 1e-06
OWNER_AXES = ("group", "dp")


def exchange(blocks):
    return lax.all_to_all(blocks, OWNER_AXES, split_axis=0, concat_axis=0, tiled=True)


def by_columns(rows, owners):
    return rows.reshape(rows.shape[0], owners, -1).transpose(1, 0, 2)


def three_terms(values):
    high = lax.reduce_precision(values, 8, 7)
    rest = values - high
    middle = lax.reduce_precision(rest, 8, 7)
    return (high, middle, rest - middle)


def build_selector(owner_list, owners, capacity):
    onehot = (owner_list[:, :, None] == jnp.arange(owners, dtype=jnp.int32)).astype(jnp.int32)
    earlier = jnp.cumsum(onehot, axis=1) - onehot
    rank_list = jnp.sum(earlier * onehot, axis=2)
    target = owner_list * capacity + rank_list
    slots = jnp.arange(owners * capacity, dtype=jnp.int32)
    return (target[:, None, :] == slots[None, :, None]).astype(jnp.bfloat16)


def local(
    teacher_hidden,
    teacher_gain,
    project_weight,
    student_hidden,
    student_gain,
    gate_weight,
    up_weight,
    down_weight,
    owner_map,
    token_ids,
    token_counts,
    id_weight,
):
    owners = lax.axis_size("group") * lax.axis_size("dp")
    tensors = lax.axis_size("tensor")
    tensor_index = lax.axis_index("tensor")
    owner_index = lax.axis_index(OWNER_AXES)
    episodes = token_counts.shape[0]
    own_span = EP_LEN // tensors
    share = own_span * episodes
    capacity = max(2, 2 * episodes // owners)
    received = owners * capacity
    student_width = student_hidden.shape[1]
    width = student_width // owners
    tokens_all = EP_LEN * episodes * owners
    teacher_width = teacher_hidden.shape[1] * tensors
    id_rows = token_ids.reshape(own_span, episodes)
    looked = jnp.sum(
        jnp.where(
            id_rows[:, :, None] == jnp.arange(id_weight.shape[0], dtype=jnp.int32)[None, None, :],
            id_weight[None, None, :],
            0.0,
        ),
        axis=2,
    )
    position = tensor_index * own_span + jnp.arange(own_span, dtype=jnp.int32)[:, None]
    token_weight = jnp.where(position < token_counts[None, :], looked, 0.0).reshape(share, 1)
    own_rows = student_hidden.astype(jnp.float32)
    own_rescale = lax.rsqrt(jnp.mean(own_rows * own_rows, axis=1, keepdims=True) + EPSILON)
    owner_rows = jnp.tile(owner_map.astype(jnp.float32), (own_span, 1))
    extras = jnp.concatenate([token_weight, owner_rows, *three_terms(own_rescale)], axis=1)
    extras = jnp.pad(extras, ((0, 0), (0, EXTRA - extras.shape[1]))).astype(jnp.bfloat16)
    arrived = exchange(
        jnp.concatenate(
            [
                by_columns(student_hidden, owners),
                jnp.broadcast_to(extras[None], (owners, share, EXTRA)),
            ],
            axis=2,
        )
    )
    rows = owners * share
    student_block = arrived[:, :, :width].reshape(rows, width).astype(jnp.float32)
    facts = arrived[:, :, width:].astype(jnp.float32)
    weight_rows = facts[:, :, 0].reshape(rows, 1)
    owner_list = facts[:, :episodes, 1].astype(jnp.int32)
    rescale = (facts[:, :, 2] + facts[:, :, 3] + facts[:, :, 4]).reshape(rows, 1)
    gain = lax.dynamic_slice_in_dim(student_gain, owner_index * width, width, 0)
    normed = (student_block * rescale * gain[None, :]).astype(jnp.bfloat16)
    gathered = lax.all_gather(normed, "tensor", axis=0, tiled=True)
    widened = teacher_hidden.astype(jnp.float32)
    squares = jnp.sum(widened * widened, axis=1)
    scaled = (widened * teacher_gain[None, :]).astype(jnp.bfloat16)
    inverse = lax.rsqrt(lax.psum(squares, "tensor") / teacher_width + EPSILON)
    summed = lax.psum_scatter(
        jnp.dot(scaled, project_weight, preferred_element_type=jnp.float32).astype(jnp.bfloat16),
        "tensor",
        scatter_dimension=0,
        tiled=True,
    ).astype(jnp.float32)
    own_inverse = lax.dynamic_slice_in_dim(inverse, tensor_index * share, share, 0)
    projected = exchange(by_columns((summed * own_inverse[:, None]).astype(jnp.bfloat16), owners))
    hidden = gate_weight.shape[1]
    gate_part = jnp.dot(gathered, gate_weight, preferred_element_type=jnp.float32)
    up_part = jnp.dot(gathered, up_weight, preferred_element_type=jnp.float32)
    parts = jnp.stack(
        [
            gate_part.astype(jnp.bfloat16).reshape(owners, -1, hidden),
            up_part.astype(jnp.bfloat16).reshape(owners, -1, hidden),
        ],
        axis=1,
    )
    sums = lax.psum_scatter(parts, OWNER_AXES, scatter_dimension=0, tiled=True).astype(jnp.float32)
    activated = (jax.nn.silu(sums[0, 0]) * sums[0, 1]).astype(jnp.bfloat16)
    act_all = lax.all_gather(activated, OWNER_AXES, axis=0, tiled=True)
    branch = jnp.dot(act_all, down_weight, preferred_element_type=jnp.float32)
    branch_local = lax.psum_scatter(
        branch.astype(jnp.bfloat16), "tensor", scatter_dimension=0, tiled=True
    ).astype(jnp.float32)
    predicted = student_block + branch_local
    difference = predicted - projected.reshape(rows, width).astype(jnp.float32)
    grad_block = (weight_rows * difference * (1.0 / math.sqrt(tokens_all))).astype(jnp.bfloat16)
    grad_all = lax.all_gather(grad_block, "tensor", axis=0, tiled=True)
    down_grad = jnp.einsum("rc,rh->ch", grad_all, act_all, preferred_element_type=jnp.float32)
    selector = build_selector(owner_list, owners, capacity)
    picked = jnp.einsum(
        "sre,spef->sprf",
        selector,
        predicted.astype(jnp.bfloat16).reshape(owners, own_span, episodes, width),
        preferred_element_type=jnp.float32,
    ).astype(jnp.bfloat16)
    outgoing = picked.reshape(owners, own_span, owners, capacity, width).transpose(2, 1, 0, 3, 4)
    incoming = exchange(outgoing.reshape(owners, own_span, received, width))
    student_out = incoming.transpose(1, 2, 0, 3).reshape(1, own_span, received, student_width)
    return (student_out, down_grad)


def solution(mesh):
    in_specs = (
        P(("group", "dp"), "tensor"),
        P("tensor"),
        P("tensor", None),
        P(("group", "dp", "tensor"), None),
        P(),
        P(("group", "dp"), "tensor"),
        P(("group", "dp"), "tensor"),
        P("tensor", ("group", "dp")),
        P(("group", "dp"), None),
        P(("group", "dp", "tensor")),
        P(("group", "dp")),
        P(),
    )
    out_specs = (P(("group", "dp"), "tensor", None, None), P(("group", "dp"), "tensor"))
    return jax.shard_map(local, mesh=mesh, in_specs=in_specs, out_specs=out_specs, check_vma=False)
```

profile of v0, /device:TPU:0, one launch (start us, length us, event | category | flops | bytes accessed | tf_op | source)
XLA Modules:
  0.0 378.6 jit_solution(4953372782439392148)
XLA Ops:
  7.2 0.0 copy-start
  7.2 1.2 multiply_reduce_fusion
  8.4 1.0 reshape.158
  9.4 0.7 eq.43
  10.2 0.8 select_reduce_fusion
  11.0 0.7 fusion.19
  11.8 0.1 select_n.26
  11.9 0.7 convert_bitcast_fusion
  12.5 0.1 tile.13
  12.6 0.1 copy.50
  12.8 0.7 pad_maximum_fusion.1
  13.5 4.2 %all-to-all-start = ((bf16[4,32,1024]{2,1,0:T(8,128)(2,1)}), bf16[4,32,1024]{2,1,0:T(8,128)(2,1)S(1)}, u32[]{:S(2)}, u32[]{:S(2)}) async-start(bf16[4,32,1024]{2,1,0:T(8,128)(2,1)} %pad_maximum_fusion.1), calls=%async_computation | async-start | bytes 524288 | tf_op jit(solution)/shard_map/all_to_all | solution.py:14
  17.8 0.8 dynamic_slice.6
  18.6 5.2 %all-to-all-done = bf16[4,32,1024]{2,1,0:T(8,128)(2,1)S(1)} async-done(((bf16[4,32,1024]{2,1,0:T(8,128)(2,1)}), bf16[4,32,1024]{2,1,0:T(8,128)(2,1)S(1)}, u32[]{:S(2)}, u32[]{:S(2)}) %all-to-all-start) | async-done | bytes 262176 | tf_op jit(solution)/shard_map/all_to_all | solution.py:14
  23.8 0.2 slice_reduce_fusion
  24.0 0.1 add.97
  24.1 0.8 fusion.8
  24.9 0.0 all-gather.4.cloned.1.call-update
  25.0 0.0 reduce-scatter.4.cloned.1.call-start
  25.0 47.4 %all-gather.4.cloned.1.call-done = bf16[1024,896]{1,0:T(8,128)(2,1)} async-done(((bf16[128,896]{1,0:T(8,128)(2,1)}), bf16[1024,896]{1,0:T(8,128)(2,1)}) %all-gather.4.cloned.1.call-update) | async-done | bytes 1835024 | tf_op jit(solution)/shard_map/all_gather | solution.py:97
  72.4 5.5 %convolution_convert_fusion.2 = bf16[1024,1184]{0,1:T(8,128)(2,1)} fusion(bf16[1024,896]{1,0:T(8,128)(2,1)} %all-gather.4.cloned.1.call-done, bf16[896,1184]{0,1:T(8,128)(2,1)S(1)} %copy-done), kind=kOutput, calls=%fused_computation.3 | convolution fusion | flops 2173861888 | bytes 6381568 | tf_op jit(solution)/shard_map/dot_general | solution.py:111
  77.9 5.7 %stack_reshape.6 = bf16[4,1,256,1184]{2,0,3,1:T(4,128)(2,1)} reshape(bf16[1024,1184]{0,1:T(8,128)(2,1)} %convolution_convert_fusion.2) | data formatting | bytes 4849664 | tf_op jit(solution)/shard_map/stack;reshape | solution.py:113
  83.6 3.6 copy.44
  87.2 4.0 %convolution_convert_fusion.1 = bf16[1024,1184]{0,1:T(8,128)(2,1)} fusion(bf16[1024,896]{1,0:T(8,128)(2,1)S(1)} %copy-done.4, bf16[896,1184]{0,1:T(8,128)(2,1)S(1)} %copy-done.3), kind=kOutput, calls=%fused_computation.2 | convolution fusion | flops 2173861888 | bytes 6381568 | tf_op jit(solution)/shard_map/dot_general | solution.py:112
  91.2 5.7 %stack_reshape.7 = bf16[4,1,256,1184]{2,0,3,1:T(4,128)(2,1)} reshape(bf16[1024,1184]{0,1:T(8,128)(2,1)} %convolution_convert_fusion.1) | data formatting | bytes 4849664 | tf_op jit(solution)/shard_map/stack;reshape | solution.py:113
  96.9 2.1 copy.45
  99.0 0.3 copy-done.1
  99.3 2.6 pad_maximum_fusion
  101.9 0.0 reduce-scatter.4.cloned.1.call-update
  101.9 0.0 all-gather.6.cloned.1.call-start
  102.0 47.6 %reduce-scatter.4.cloned.1.call-done = bf16[1,2,256,1184]{2,3,1,0:T(8,128)(2,1)} async-done(((bf16[4,2,256,1184]{2,3,1,0:T(8,128)(2,1)}), bf16[1,2,256,1184]{2,3,1,0:T(8,128)(2,1)}) %reduce-scatter.4.cloned.1.call-update) | async-done | bytes 1212432 | tf_op jit(solution)/shard_map/reduce_scatter | solution.py:120
  149.6 1.4 convert_element_type.93
  151.1 1.2 fusion.2
  152.3 0.0 all-gather.6.cloned.1.call-update
  152.3 0.0 reduce-scatter.8.cloned.1.call-start
  152.3 6.4 %convolution_convert_fusion = bf16[256,3584]{1,0:T(8,128)(2,1)} fusion(bf16[1024,3584]{1,0:T(8,128)(2,1)} %param.14, bf16[256,1024]{1,0:T(8,128)(2,1)S(1)} %copy-done.2, f32[1024]{0:T(1024)S(1)} %copy-done.5), kind=kOutput, calls=%fused_computation | convolution fusion | flops 1880752128 | bytes 9703424 | tf_op jit(solution)/shard_map/dot_general | solution.py:103
  158.7 0.0 reduce-scatter.8.cloned.1.call-update
  158.7 0.0 reduce-scatter.6.cloned.1.call-start
  158.8 18.4 %all-gather.6.cloned.1.call-done = bf16[1024,1184]{0,1:T(8,128)(2,1)} async-done(((bf16[256,1184]{0,1:T(8,128)(2,1)}), bf16[1024,1184]{0,1:T(8,128)(2,1)}) %all-gather.6.cloned.1.call-update) | async-done | bytes 2424848 | tf_op jit(solution)/shard_map/all_gather | solution.py:122
  177.1 6.5 %convolution_convert_fusion.3 = bf16[1024,896]{1,0:T(8,128)(2,1)} fusion(bf16[1024,1184]{0,1:T(8,128)(2,1)} %all-gather.6.cloned.1.call-done, bf16[1184,896]{1,0:T(8,128)(2,1)} %param.19), kind=kOutput, calls=%fused_computation.4 | convolution fusion | flops 2173566976 | bytes 6381568 | tf_op jit(solution)/shard_map/dot_general | solution.py:123
  183.6 0.0 reduce-scatter.6.cloned.1.call-update
  183.7 0.2 fusion.4
  183.8 21.4 %psum.7 = f32[256]{0:T(256)S(1)} all-reduce(f32[256]{0:T(256)S(1)} %fusion.4), channel_id=1, replica_groups=mesh['group'=2,'dp'=2,'tensor'=8] {'tensor'}, use_global_device_ids=true, to_apply=%region_8.9 | all-reduce | flops 256 | bytes 2048 | tf_op jit(solution)/shard_map/psum | solution.py:101
  205.2 0.1 dynamic_slice.7
  205.3 41.9 %reduce-scatter.8.cloned.1.call-done = bf16[32,3584]{1,0:T(8,128)(2,1)} async-done(((bf16[256,3584]{1,0:T(8,128)(2,1)}), bf16[32,3584]{1,0:T(8,128)(2,1)}) %reduce-scatter.8.cloned.1.call-update) | async-done | bytes 229392 | tf_op jit(solution)/shard_map/reduce_scatter | solution.py:102
  247.2 1.0 multiply_convert_fusion
  248.3 0.7 copy.55
  249.0 3.4 all-to-all-start.2
  252.4 0.2 all-gather.8.cloned.1.call-start
  252.6 0.1 mul.103
  252.7 5.3 %all-to-all-done.2 = bf16[4,32,896]{2,1,0:T(8,128)(2,1)S(1)} async-done(((bf16[4,32,896]{2,1,0:T(8,128)(2,1)}), bf16[4,32,896]{2,1,0:T(8,128)(2,1)S(1)}, u32[]{:S(2)}, u32[]{:S(2)}) %all-to-all-start.2) | async-done | bytes 229408 | tf_op jit(solution)/shard_map/all_to_all | solution.py:14
  258.0 58.9 %reduce-scatter.6.cloned.1.call-done = bf16[128,896]{1,0:T(8,128)(2,1)} async-done(((bf16[1024,896]{1,0:T(8,128)(2,1)}), bf16[128,896]{1,0:T(8,128)(2,1)}) %reduce-scatter.6.cloned.1.call-update) | async-done | bytes 229392 | tf_op jit(solution)/shard_map/reduce_scatter | solution.py:124
  316.8 1.8 fusion.11
  318.6 0.0 all-gather.8.cloned.1.call-update
  318.6 0.3 fusion.17
  318.9 0.1 fusion.14
  319.0 0.1 reduce_window_sum.11
  319.0 0.2 select_reduce_fusion.1
  319.3 0.4 fusion
  319.7 10.6 %all_to_all.15 = bf16[4,2,32,896]{3,2,1,0:T(8,128)(2,1)S(1)} all-to-all(bf16[4,2,32,896]{3,2,1,0:T(8,128)(2,1)S(1)} %bitcast.65), channel_id=1, replica_groups=mesh['group'=2,'dp'=2,'tensor'=8] {'group','dp'}, dimensions={0} | all-to-all | bytes 917504 | tf_op jit(solution)/shard_map/all_to_all | solution.py:14
  330.3 0.4 copy.47
  330.7 0.9 reshape.162
  331.6 33.1 %all-gather.8.cloned.1.call-done = bf16[1024,896]{1,0:T(8,128)(2,1)} async-done(((bf16[128,896]{1,0:T(8,128)(2,1)}), bf16[1024,896]{1,0:T(8,128)(2,1)}) %all-gather.8.cloned.1.call-update) | async-done | bytes 1835024 | tf_op jit(solution)/shard_map/all_gather | solution.py:130
  364.8 6.9 %fusion.21 = f32[896,1184]{0,1:T(8,128)} fusion(bf16[1024,1184]{0,1:T(8,128)(2,1)} %all-gather.6.cloned.1.call-done, bf16[1024,896]{1,0:T(8,128)(2,1)} %all-gather.8.cloned.1.call-done), kind=kOutput, calls=%fused_computation.57 | convolution fusion | flops 2172649472 | bytes 8503296 | tf_op jit(solution)/shard_map/rc,rh->ch/dot_general | solution.py:131
  (23 shorter events, 0.2 us)
Async XLA Ops:
  7.2 65.3 %copy-start = (bf16[896,1184]{0,1:T(8,128)(2,1)S(1)}, bf16[896,1184]{0,1:T(8,128)(2,1)}, u32[]{:S(2)}) copy-start(bf16[896,1184]{0,1:T(8,128)(2,1)} %param.17) | copy-start | bytes 6365188
  13.5 10.2 %all-to-all-start = ((bf16[4,32,1024]{2,1,0:T(8,128)(2,1)}), bf16[4,32,1024]{2,1,0:T(8,128)(2,1)S(1)}, u32[]{:S(2)}, u32[]{:S(2)}) async-start(bf16[4,32,1024]{2,1,0:T(8,128)(2,1)} %pad_maximum_fusion.1), calls=%async_computation | async-start | bytes 524288 | tf_op jit(solution)/shard_map/all_to_all | solution.py:14
  17.8 54.7 %all-gather.4.cloned.1.call-start = ((), (), s32[]{:S(2)}) async-start(), calls=%async_computation.6 | async-start | bytes 2064384 | tf_op jit(solution)/shard_map/all_gather | solution.py:97
  25.0 124.6 %reduce-scatter.4.cloned.1.call-start = ((), (), s32[]{:S(2)}) async-start(), calls=%async_computation.7 | async-start | bytes 6062080 | tf_op jit(solution)/shard_map/reduce_scatter | solution.py:120
  83.6 3.6 copy-start.3
  83.6 3.6 copy-start.4
  96.9 2.4 copy-start.1
  101.9 75.2 %all-gather.6.cloned.1.call-start = ((), (), s32[]{:S(2)}) async-start(), calls=%async_computation.8 | async-start | bytes 3031040 | tf_op jit(solution)/shard_map/all_gather | solution.py:122
  151.0 1.3 copy-start.2
  151.1 1.3 copy-start.5
  152.3 94.9 %reduce-scatter.8.cloned.1.call-start = ((), (), s32[]{:S(2)}) async-start(), calls=%async_computation.10 | async-start | bytes 2064384 | tf_op jit(solution)/shard_map/reduce_scatter | solution.py:102
  158.7 158.1 %reduce-scatter.6.cloned.1.call-start = ((), (), s32[]{:S(2)}) async-start(), calls=%async_computation.9 | async-start | bytes 2064384 | tf_op jit(solution)/shard_map/reduce_scatter | solution.py:124
  249.0 9.0 %all-to-all-start.2 = ((bf16[4,32,896]{2,1,0:T(8,128)(2,1)}), bf16[4,32,896]{2,1,0:T(8,128)(2,1)S(1)}, u32[]{:S(2)}, u32[]{:S(2)}) async-start(bf16[4,32,896]{2,1,0:T(8,128)(2,1)} %bitcast.64), calls=%async_computation.5 | async-start | bytes 458752 | tf_op jit(solution)/shard_map/all_to_all | solution.py:14
  252.4 112.4 %all-gather.8.cloned.1.call-start = ((), (), s32[]{:S(2)}) async-start(), calls=%async_computation.11 | async-start | bytes 2064384 | tf_op jit(solution)/shard_map/all_gather | solution.py:130
Sparse Core Ops, SparseCore 0:
  25.1 47.3 all-gather.3
  102.0 47.4 reduce-scatter.3
  152.4 24.7 all-gather.5
  180.5 66.7 reduce-scatter.7
  251.1 65.6 reduce-scatter.5
  319.5 45.2 all-gather.7
where the time goes:
time: 379 us
  waiting for transfers between devices  258 us (68%)
  blocking collectives  32 us (8%)
  matrix products  29.6 us (8%)
  local copies, waits for them, and re-layouts  22.6 us (6%)
  between operations  14.3 us (4%)
  other arithmetic  14.1 us (4%)
  starting transfers between devices  8.01 us (2%)
    reduce_scatter x1, waiting for transfers between devices, local(): lax.psum_scatter(branch.astype(jnp.bfloat16), 'tensor', scatter_dimension...  58.9 us
    reduce_scatter x1, waiting for transfers between devices, local(): lax.psum_scatter(parts, OWNER_AXES, scatter_dimension=0, tiled=True)  47.6 us
    all_gather x1, waiting for transfers between devices, local(): gathered = lax.all_gather(normed, 'tensor', axis=0, tiled=True)  47.4 us
    reduce_scatter x1, waiting for transfers between devices, local(): lax.psum_scatter(jnp.dot(scaled, project_weight, preferred_element_type=j...  41.9 us
    all_gather x1, waiting for transfers between devices, local(): grad_all = lax.all_gather(grad_block, 'tensor', axis=0, tiled=True)  33.1 us
    psum x1, blocking collectives, local(): inverse = lax.rsqrt(lax.psum(squares, 'tensor') / teacher_width + EPSILON)  21.4 us
    all_gather x1, waiting for transfers between devices, local(): act_all = lax.all_gather(activated, OWNER_AXES, axis=0, tiled=True)  18.4 us
    another operation x4, local copies, waits for them, and re-layouts, local(): jnp.stack([gate_part.astype(jnp.bfloat16).reshape(owners, -1, hidden), up...  17.2 us
  transfers between devices with their start and end apart: 8, of which 8 were waited for; matrix products, arithmetic and copies ran while one was open for 5% of the time, Pallas kernels for 0%

commit v1 on v0

--- a/solution.py
+++ b/solution.py
@@ -127,8 +127,22 @@
     predicted = student_block + branch_local
     difference = predicted - projected.reshape(rows, width).astype(jnp.float32)
     grad_block = (weight_rows * difference * (1.0 / math.sqrt(tokens_all))).astype(jnp.bfloat16)
-    grad_all = lax.all_gather(grad_block, "tensor", axis=0, tiled=True)
-    down_grad = jnp.einsum("rc,rh->ch", grad_all, act_all, preferred_element_type=jnp.float32)
+    size, index, rows_2 = (lax.axis_size("tensor"), lax.axis_index("tensor"), grad_block.shape[0])
+    upward = [(i, (i + 1) % size) for i in range(size)]
+    block, total = (grad_block, None)
+    for hop in range(size):
+        coming = lax.ppermute(block, "tensor", upward) if hop < size - 1 else None
+        update = jnp.einsum(
+            "rc,rh->ch",
+            block,
+            lax.dynamic_slice_in_dim(
+                act_all, (index - hop) % size * rows_2, block.shape[0], axis=0
+            ),
+            preferred_element_type=jnp.float32,
+        )
+        total = update if total is None else total + update
+        block = coming
+    down_grad = total
     selector = build_selector(owner_list, owners, capacity)
     picked = jnp.einsum(
         "sre,spef->sprf",

time: 379 us -> 397 us (1.047)
  waiting for transfers between devices: 258 us -> 275 us
  blocking collectives: 32 us -> 21.5 us
  matrix products: 29.6 us -> 36.6 us
  starting transfers between devices: 8.01 us -> 12.3 us
    ppermute x0 -> x7, waiting for transfers between devices: none -> 51.1 us  [local(): coming = lax.ppermute(block, 'tensor', upward) if hop < size - 1 else None]
    all_gather x1 -> x0, waiting for transfers between devices: 33.1 us -> none  [local(): grad_all = lax.all_gather(grad_block, 'tensor', axis=0, tiled=True)]
    all_to_all x1 -> x0, blocking collectives: 10.6 us -> none  [exchange(): lax.all_to_all(blocks, OWNER_AXES, split_axis=0, concat_axis=0, tiled=True)]
    dot_general x1 -> x8, matrix products: 6.93 us -> 13.9 us  [local(): jnp.einsum('rc,rh->ch', block, lax.dynamic_slice_in_dim(act_all, (index -...]
    all_to_all x2 -> x3, starting transfers between devices: 7.62 us -> 11.3 us  [exchange(): lax.all_to_all(blocks, OWNER_AXES, split_axis=0, concat_axis=0, tiled=True)]
    all_to_all x2 -> x3, waiting for transfers between devices: 10.5 us -> 10.2 us  [exchange(): lax.all_to_all(blocks, OWNER_AXES, split_axis=0, concat_axis=0, tiled=True)]
  transfers between devices with their start and end apart: 8 -> 15, of which waited for: 8 -> 14; matrix products, arithmetic and copies ran while one was open for 5% -> 7% of each run, Pallas kernels for 0% -> 0%
where the time goes in v1:
time: 397 us; the launch traced here: 396 us
  waiting for transfers between devices  275 us (69%)
  matrix products  36.6 us (9%)
  local copies, waits for them, and re-layouts  23.4 us (6%)
  blocking collectives  21.5 us (5%)
  between operations  14.1 us (4%)
  other arithmetic  13.4 us (3%)
  starting transfers between devices  12.3 us (3%)
    reduce_scatter x1, waiting for transfers between devices, local(): lax.psum_scatter(branch.astype(jnp.bfloat16), 'tensor', scatter_dimension...  58.7 us
    ppermute x7, waiting for transfers between devices, local(): coming = lax.ppermute(block, 'tensor', upward) if hop < size - 1 else None  51.1 us
    reduce_scatter x1, waiting for transfers between devices, local(): lax.psum_scatter(parts, OWNER_AXES, scatter_dimension=0, tiled=True)  47.6 us
    all_gather x1, waiting for transfers between devices, local(): gathered = lax.all_gather(normed, 'tensor', axis=0, tiled=True)  47.4 us
    reduce_scatter x1, waiting for transfers between devices, local(): lax.psum_scatter(jnp.dot(scaled, project_weight, preferred_element_type=j...  41.3 us
    psum x1, blocking collectives, local(): inverse = lax.rsqrt(lax.psum(squares, 'tensor') / teacher_width + EPSILON)  21.5 us
    all_gather x1, waiting for transfers between devices, local(): act_all = lax.all_gather(activated, OWNER_AXES, axis=0, tiled=True)  18.4 us
    another operation x4, local copies, waits for them, and re-layouts, local(): jnp.stack([gate_part.astype(jnp.bfloat16).reshape(owners, -1, hidden), up...  17.2 us
  transfers between devices with their start and end apart: 15, of which 14 were waited for; matrix products, arithmetic and copies ran while one was open for 7% of the time, Pallas kernels for 0%

profile of v1, /device:TPU:0, one launch (start us, length us, event | category | flops | bytes accessed | tf_op | source)
XLA Modules:
  0.0 396.3 jit_solution(5200581541820296720)
XLA Ops:
  7.2 1.2 multiply_reduce_fusion
  8.4 1.0 reshape.158
  9.4 0.7 eq.52
  10.2 0.8 select_reduce_fusion
  11.0 0.7 fusion.36
  11.7 0.1 select_n.85
  11.8 0.7 convert_bitcast_fusion
  12.5 0.1 tile.13
  12.6 0.1 copy.50
  12.8 0.7 pad_maximum_fusion.1
  13.5 4.2 %all-to-all-start = ((bf16[4,32,1024]{2,1,0:T(8,128)(2,1)}), bf16[4,32,1024]{2,1,0:T(8,128)(2,1)S(1)}, u32[]{:S(2)}, u32[]{:S(2)}) async-start(bf16[4,32,1024]{2,1,0:T(8,128)(2,1)} %pad_maximum_fusion.1), calls=%async_computation | async-start | bytes 524288 | tf_op jit(solution)/shard_map/all_to_all | solution.py:14
  17.8 0.8 dynamic_slice.30
  18.5 5.2 %all-to-all-done = bf16[4,32,1024]{2,1,0:T(8,128)(2,1)S(1)} async-done(((bf16[4,32,1024]{2,1,0:T(8,128)(2,1)}), bf16[4,32,1024]{2,1,0:T(8,128)(2,1)S(1)}, u32[]{:S(2)}, u32[]{:S(2)}) %all-to-all-start) | async-done | bytes 262176 | tf_op jit(solution)/shard_map/all_to_all | solution.py:14
  23.8 0.2 slice_reduce_fusion
  24.0 0.1 add.174
  24.1 0.8 fusion.8
  25.0 47.4 %all-gather.3.cloned.1.call-done = bf16[1024,896]{1,0:T(8,128)(2,1)} async-done(((bf16[128,896]{1,0:T(8,128)(2,1)}), bf16[1024,896]{1,0:T(8,128)(2,1)}) %all-gather.3.cloned.1.call-update) | async-done | bytes 1835024 | tf_op jit(solution)/shard_map/all_gather | solution.py:97
  72.4 5.5 %convolution_convert_fusion.1 = bf16[1024,1184]{0,1:T(8,128)(2,1)} fusion(bf16[1024,896]{1,0:T(8,128)(2,1)} %all-gather.3.cloned.1.call-done, bf16[896,1184]{0,1:T(8,128)(2,1)S(1)} %copy-done), kind=kOutput, calls=%fused_computation.9 | convolution fusion | flops 2173861888 | bytes 6381568 | tf_op jit(solution)/shard_map/dot_general | solution.py:112
  77.9 5.7 %stack_reshape.7 = bf16[4,1,256,1184]{2,0,3,1:T(4,128)(2,1)} reshape(bf16[1024,1184]{0,1:T(8,128)(2,1)} %convolution_convert_fusion.1) | data formatting | bytes 4849664 | tf_op jit(solution)/shard_map/stack;reshape | solution.py:113
  83.6 3.6 copy.45
  87.2 4.0 %convolution_convert_fusion.2 = bf16[1024,1184]{0,1:T(8,128)(2,1)} fusion(bf16[1024,896]{1,0:T(8,128)(2,1)S(1)} %copy-done.6, bf16[896,1184]{0,1:T(8,128)(2,1)S(1)} %copy-done.5), kind=kOutput, calls=%fused_computation.10 | convolution fusion | flops 2173861888 | bytes 6381568 | tf_op jit(solution)/shard_map/dot_general | solution.py:111
  91.2 5.7 %stack_reshape.6 = bf16[4,1,256,1184]{2,0,3,1:T(4,128)(2,1)} reshape(bf16[1024,1184]{0,1:T(8,128)(2,1)} %convolution_convert_fusion.2) | data formatting | bytes 4849664 | tf_op jit(solution)/shard_map/stack;reshape | solution.py:113
  96.9 2.1 copy.44
  99.1 0.3 copy-done.2
  99.3 2.6 pad_maximum_fusion
  102.0 47.6 %reduce-scatter.4.cloned.1.call-done = bf16[1,2,256,1184]{2,3,1,0:T(8,128)(2,1)} async-done(((bf16[4,2,256,1184]{2,3,1,0:T(8,128)(2,1)}), bf16[1,2,256,1184]{2,3,1,0:T(8,128)(2,1)}) %reduce-scatter.4.cloned.1.call-update) | async-done | bytes 1212432 | tf_op jit(solution)/shard_map/reduce_scatter | solution.py:120
  149.6 1.4 convert_element_type.93
  151.1 1.2 fusion.2
  152.3 6.4 %convolution_convert_fusion = bf16[256,3584]{1,0:T(8,128)(2,1)} fusion(bf16[1024,3584]{1,0:T(8,128)(2,1)} %param.14, bf16[256,1024]{1,0:T(8,128)(2,1)S(1)} %copy-done.4, f32[1024]{0:T(1024)S(1)} %copy-done.7), kind=kOutput, calls=%fused_computation | convolution fusion | flops 1880752128 | bytes 9703424 | tf_op jit(solution)/shard_map/dot_general | solution.py:103
  158.8 18.4 %all-gather.5.cloned.1.call-done = bf16[1024,1184]{0,1:T(8,128)(2,1)} async-done(((bf16[256,1184]{0,1:T(8,128)(2,1)}), bf16[1024,1184]{0,1:T(8,128)(2,1)}) %all-gather.5.cloned.1.call-update) | async-done | bytes 2424848 | tf_op jit(solution)/shard_map/all_gather | solution.py:122
  177.1 6.5 %convolution_convert_fusion.3 = bf16[1024,896]{1,0:T(8,128)(2,1)} fusion(bf16[1024,1184]{0,1:T(8,128)(2,1)} %all-gather.5.cloned.1.call-done, bf16[1184,896]{1,0:T(8,128)(2,1)} %param.19), kind=kOutput, calls=%fused_computation.11 | convolution fusion | flops 2173566976 | bytes 6381568 | tf_op jit(solution)/shard_map/dot_general | solution.py:123
  183.8 0.2 fusion.4
  184.0 21.5 %psum.7 = f32[256]{0:T(256)S(1)} all-reduce(f32[256]{0:T(256)S(1)} %fusion.4), channel_id=1, replica_groups=mesh['group'=2,'dp'=2,'tensor'=8] {'tensor'}, use_global_device_ids=true, to_apply=%region_8.9 | all-reduce | flops 256 | bytes 2048 | tf_op jit(solution)/shard_map/psum | solution.py:101
  205.6 0.3 fusion.26
  205.9 41.3 %reduce-scatter.8.cloned.1.call-done = bf16[32,3584]{1,0:T(8,128)(2,1)} async-done(((bf16[256,3584]{1,0:T(8,128)(2,1)}), bf16[32,3584]{1,0:T(8,128)(2,1)}) %reduce-scatter.8.cloned.1.call-update) | async-done | bytes 229392 | tf_op jit(solution)/shard_map/reduce_scatter | solution.py:102
  247.2 1.0 multiply_convert_fusion
  248.3 0.7 copy.55
  249.0 3.6 all-to-all-start.2
  252.6 0.1 mul.127
  252.7 0.2 select_reduce_fusion.1
  253.0 5.0 %all-to-all-done.2 = bf16[4,32,896]{2,1,0:T(8,128)(2,1)S(1)} async-done(((bf16[4,32,896]{2,1,0:T(8,128)(2,1)}), bf16[4,32,896]{2,1,0:T(8,128)(2,1)S(1)}, u32[]{:S(2)}, u32[]{:S(2)}) %all-to-all-start.2) | async-done | bytes 229408 | tf_op jit(solution)/shard_map/all_to_all | solution.py:14
  258.0 58.7 %reduce-scatter.6.cloned.1.call-done = bf16[128,896]{1,0:T(8,128)(2,1)} async-done(((bf16[1024,896]{1,0:T(8,128)(2,1)}), bf16[128,896]{1,0:T(8,128)(2,1)}) %reduce-scatter.6.cloned.1.call-update) | async-done | bytes 229392 | tf_op jit(solution)/shard_map/reduce_scatter | solution.py:124
  316.7 1.1 fusion.11
  317.8 0.4 fusion
  318.2 0.8 copy.54
  319.0 3.5 all-to-all-start.1
  322.5 0.9 collective-permute-start
  323.4 1.7 fusion.20
  325.0 8.1 %collective-permute-done = bf16[128,896]{1,0:T(8,128)(2,1)S(1)} collective-permute-done((bf16[128,896]{1,0:T(8,128)(2,1)S(1)}, bf16[128,896]{1,0:T(8,128)(2,1)S(1)}, u32[]{:S(2)}, u32[]{:S(2)}) %collective-permute-start) | collective-permute-done | bytes 229408 | tf_op jit(solution)/shard_map/ppermute | solution.py:134
  333.2 3.7 convolution_add_fusion.6
  336.9 0.4 copy.47
  337.2 0.9 reshape.162
  338.2 4.8 %collective-permute-done.1 = bf16[128,896]{1,0:T(8,128)(2,1)S(1)} collective-permute-done((bf16[128,896]{1,0:T(8,128)(2,1)S(1)}, bf16[128,896]{1,0:T(8,128)(2,1)S(1)}, u32[]{:S(2)}, u32[]{:S(2)}) %collective-permute-start.1) | collective-permute-done | bytes 229408 | tf_op jit(solution)/shard_map/ppermute | solution.py:134
  342.9 3.0 convolution_add_fusion.5
  345.9 5.9 %collective-permute-done.2 = bf16[128,896]{1,0:T(8,128)(2,1)S(1)} collective-permute-done((bf16[128,896]{1,0:T(8,128)(2,1)S(1)}, bf16[128,896]{1,0:T(8,128)(2,1)S(1)}, u32[]{:S(2)}, u32[]{:S(2)}) %collective-permute-start.2) | collective-permute-done | bytes 229408 | tf_op jit(solution)/shard_map/ppermute | solution.py:134
  351.8 0.7 convolution_add_fusion.4
  352.6 8.0 %collective-permute-done.3 = bf16[128,896]{1,0:T(8,128)(2,1)S(1)} collective-permute-done((bf16[128,896]{1,0:T(8,128)(2,1)S(1)}, bf16[128,896]{1,0:T(8,128)(2,1)S(1)}, u32[]{:S(2)}, u32[]{:S(2)}) %collective-permute-start.3) | collective-permute-done | bytes 229408 | tf_op jit(solution)/shard_map/ppermute | solution.py:134
  360.6 0.7 convolution_add_fusion.3
  361.3 8.0 %collective-permute-done.4 = bf16[128,896]{1,0:T(8,128)(2,1)S(1)} collective-permute-done((bf16[128,896]{1,0:T(8,128)(2,1)S(1)}, bf16[128,896]{1,0:T(8,128)(2,1)S(1)}, u32[]{:S(2)}, u32[]{:S(2)}) %collective-permute-start.4) | collective-permute-done | bytes 229408 | tf_op jit(solution)/shard_map/ppermute | solution.py:134
  369.3 0.7 convolution_add_fusion.2
  370.0 8.3 %collective-permute-done.5 = bf16[128,896]{1,0:T(8,128)(2,1)S(1)} collective-permute-done((bf16[128,896]{1,0:T(8,128)(2,1)S(1)}, bf16[128,896]{1,0:T(8,128)(2,1)S(1)}, u32[]{:S(2)}, u32[]{:S(2)}) %collective-permute-start.5) | collective-permute-done | bytes 229408 | tf_op jit(solution)/shard_map/ppermute | solution.py:134
  378.3 0.7 convolution_add_fusion.1
  379.0 8.0 %collective-permute-done.6 = bf16[128,896]{1,0:T(8,128)(2,1)S(1)} collective-permute-done((bf16[128,896]{1,0:T(8,128)(2,1)S(1)}, bf16[128,896]{1,0:T(8,128)(2,1)S(1)}, u32[]{:S(2)}, u32[]{:S(2)}) %collective-permute-start.6) | collective-permute-done | bytes 229408 | tf_op jit(solution)/shard_map/ppermute | solution.py:134
  387.0 2.7 convolution_add_fusion
  (46 shorter events, 0.6 us)
Async XLA Ops:
  7.2 65.3 %copy-start = (bf16[896,1184]{0,1:T(8,128)(2,1)S(1)}, bf16[896,1184]{0,1:T(8,128)(2,1)}, u32[]{:S(2)}) copy-start(bf16[896,1184]{0,1:T(8,128)(2,1)} %param.18) | copy-start | bytes 6365188
  13.5 10.2 %all-to-all-start = ((bf16[4,32,1024]{2,1,0:T(8,128)(2,1)}), bf16[4,32,1024]{2,1,0:T(8,128)(2,1)S(1)}, u32[]{:S(2)}, u32[]{:S(2)}) async-start(bf16[4,32,1024]{2,1,0:T(8,128)(2,1)} %pad_maximum_fusion.1), calls=%async_computation | async-start | bytes 524288 | tf_op jit(solution)/shard_map/all_to_all | solution.py:14
  17.8 54.7 %all-gather.3.cloned.1.call-start = ((), (), s32[]{:S(2)}) async-start(), calls=%async_computation.6 | async-start | bytes 2064384 | tf_op jit(solution)/shard_map/all_gather | solution.py:97
  24.9 124.6 %reduce-scatter.4.cloned.1.call-start = ((), (), s32[]{:S(2)}) async-start(), calls=%async_computation.7 | async-start | bytes 6062080 | tf_op jit(solution)/shard_map/reduce_scatter | solution.py:120
  83.6 3.6 copy-start.5
  83.6 3.6 copy-start.6
  96.9 2.4 copy-start.2
  101.9 75.2 %all-gather.5.cloned.1.call-start = ((), (), s32[]{:S(2)}) async-start(), calls=%async_computation.8 | async-start | bytes 3031040 | tf_op jit(solution)/shard_map/all_gather | solution.py:122
  151.0 1.3 copy-start.4
  151.0 1.3 copy-start.7
  152.3 94.9 %reduce-scatter.8.cloned.1.call-start = ((), (), s32[]{:S(2)}) async-start(), calls=%async_computation.10 | async-start | bytes 2064384 | tf_op jit(solution)/shard_map/reduce_scatter | solution.py:102
  158.7 158.0 %reduce-scatter.6.cloned.1.call-start = ((), (), s32[]{:S(2)}) async-start(), calls=%async_computation.9 | async-start | bytes 2064384 | tf_op jit(solution)/shard_map/reduce_scatter | solution.py:124
  249.0 9.0 %all-to-all-start.2 = ((bf16[4,32,896]{2,1,0:T(8,128)(2,1)}), bf16[4,32,896]{2,1,0:T(8,128)(2,1)S(1)}, u32[]{:S(2)}, u32[]{:S(2)}) async-start(bf16[4,32,896]{2,1,0:T(8,128)(2,1)} %bitcast.70), calls=%async_computation.5 | async-start | bytes 458752 | tf_op jit(solution)/shard_map/all_to_all | solution.py:14
  319.0 17.9 %all-to-all-start.1 = ((bf16[4,2,32,896]{3,2,1,0:T(8,128)(2,1)}), bf16[4,2,32,896]{3,2,1,0:T(8,128)(2,1)S(1)}, u32[]{:S(2)}, u32[]{:S(2)}) async-start(bf16[4,2,32,896]{3,2,1,0:T(8,128)(2,1)} %bitcast.68), calls=%async_computation.3 | async-start | bytes 917504 | tf_op jit(solution)/shard_map/all_to_all | solution.py:14
  322.5 10.7 %collective-permute-start = (bf16[128,896]{1,0:T(8,128)(2,1)S(1)}, bf16[128,896]{1,0:T(8,128)(2,1)S(1)}, u32[]{:S(2)}, u32[]{:S(2)}) collective-permute-start(bf16[128,896]{1,0:T(8,128)(2,1)S(1)} %get-tuple-element.6), channel_id=1, source_target_pairs={{0,1},{1,2},{2,3},{3,4},{4,5},{5,6},{6,7},{7,0},{8,9},{9,10},{10,1... | collective-permute-start | bytes 688136 | tf_op jit(solution)/shard_map/ppermute | solution.py:134
  333.2 9.8 %collective-permute-start.1 = (bf16[128,896]{1,0:T(8,128)(2,1)S(1)}, bf16[128,896]{1,0:T(8,128)(2,1)S(1)}, u32[]{:S(2)}, u32[]{:S(2)}) collective-permute-start(bf16[128,896]{1,0:T(8,128)(2,1)S(1)} %collective-permute-done), channel_id=1, source_target_pairs={{0,1},{1,2},{2,3},{3,4},{4,5},{5,6},{6,7},{7,0},{8,9},{9,10},{10,1... | collective-permute-start | bytes 688136 | tf_op jit(solution)/shard_map/ppermute | solution.py:134
  338.2 13.7 %copy-start.3 = (bf16[1024,1184]{0,1:T(8,128)(2,1)S(1)}, bf16[1024,1184]{0,1:T(8,128)(2,1)}, u32[]{:S(2)}) copy-start(bf16[1024,1184]{0,1:T(8,128)(2,1)} %all-gather.5.cloned.1.call-done) | copy-start | bytes 7274500
  342.9 8.9 %collective-permute-start.2 = (bf16[128,896]{1,0:T(8,128)(2,1)S(1)}, bf16[128,896]{1,0:T(8,128)(2,1)S(1)}, u32[]{:S(2)}, u32[]{:S(2)}) collective-permute-start(bf16[128,896]{1,0:T(8,128)(2,1)S(1)} %collective-permute-done.1), channel_id=1, source_target_pairs={{0,1},{1,2},{2,3},{3,4},{4,5},{5,6},{6,7},{7,0},{8,9},{9,10},{10,1... | collective-permute-start | bytes 688136 | tf_op jit(solution)/shard_map/ppermute | solution.py:134
  351.8 8.7 %collective-permute-start.3 = (bf16[128,896]{1,0:T(8,128)(2,1)S(1)}, bf16[128,896]{1,0:T(8,128)(2,1)S(1)}, u32[]{:S(2)}, u32[]{:S(2)}) collective-permute-start(bf16[128,896]{1,0:T(8,128)(2,1)S(1)} %collective-permute-done.2), channel_id=1, source_target_pairs={{0,1},{1,2},{2,3},{3,4},{4,5},{5,6},{6,7},{7,0},{8,9},{9,10},{10,1... | collective-permute-start | bytes 688136 | tf_op jit(solution)/shard_map/ppermute | solution.py:134
  360.6 8.7 %collective-permute-start.4 = (bf16[128,896]{1,0:T(8,128)(2,1)S(1)}, bf16[128,896]{1,0:T(8,128)(2,1)S(1)}, u32[]{:S(2)}, u32[]{:S(2)}) collective-permute-start(bf16[128,896]{1,0:T(8,128)(2,1)S(1)} %collective-permute-done.3), channel_id=1, source_target_pairs={{0,1},{1,2},{2,3},{3,4},{4,5},{5,6},{6,7},{7,0},{8,9},{9,10},{10,1... | collective-permute-start | bytes 688136 | tf_op jit(solution)/shard_map/ppermute | solution.py:134
  369.3 9.0 %collective-permute-start.5 = (bf16[128,896]{1,0:T(8,128)(2,1)S(1)}, bf16[128,896]{1,0:T(8,128)(2,1)S(1)}, u32[]{:S(2)}, u32[]{:S(2)}) collective-permute-start(bf16[128,896]{1,0:T(8,128)(2,1)S(1)} %collective-permute-done.4), channel_id=1, source_target_pairs={{0,1},{1,2},{2,3},{3,4},{4,5},{5,6},{6,7},{7,0},{8,9},{9,10},{10,1... | collective-permute-start | bytes 688136 | tf_op jit(solution)/shard_map/ppermute | solution.py:134
  378.3 8.7 %collective-permute-start.6 = (bf16[128,896]{1,0:T(8,128)(2,1)S(1)}, bf16[128,896]{1,0:T(8,128)(2,1)S(1)}, u32[]{:S(2)}, u32[]{:S(2)}) collective-permute-start(bf16[128,896]{1,0:T(8,128)(2,1)S(1)} %collective-permute-done.5), channel_id=1, source_target_pairs={{0,1},{1,2},{2,3},{3,4},{4,5},{5,6},{6,7},{7,0},{8,9},{9,10},{10,1... | collective-permute-start | bytes 688136 | tf_op jit(solution)/shard_map/ppermute | solution.py:134
  378.3 11.5 %copy-start.1 = (bf16[896,1184]{0,1:T(8,128)(2,1)S(1)}, bf16[896,1184]{0,1:T(8,128)(2,1)}, u32[]{:S(2)}) copy-start(bf16[896,1184]{0,1:T(8,128)(2,1)} %param.18) | copy-start | bytes 6365188
Sparse Core Ops, SparseCore 0:
  25.1 47.3 all-gather.2
  102.0 47.4 reduce-scatter.3
  152.4 24.6 all-gather.4
  180.4 66.7 reduce-scatter.7
  251.1 65.5 reduce-scatter.5
